TPU v7x, 32 devices: a whole 2x2x4 slice. The times are simulated.
32 devices in a mesh: section: 4 (over y, core), tensor: 2 (over x), dp: 4 (over z).
Axes of the slice: x: 2, y: 2, z: 4, core: 2. Of those that a mesh axis runs over, the one named last changes fastest.
Arguments:
- acts: bfloat16 [4, 8, 256, 2048], P('section', 'dp', 'tensor'), parts along dimension 1, may hold values from -6 to 6
- fresh: bfloat16 [8, 256, 2048], P('dp', 'tensor'), parts along dimension 0, may hold values from -6 to 6
- order: int32 [4, 2], P('section'), may hold values from 0 to 1
- ln_gain: float32 [4, 2048], P('section'), may hold values from 0.1 to 1.9
- ln_bias: float32 [4, 2048], P('section'), may hold values from -3 to 3
- wqkv: bfloat16 [4, 2048, 6144], P('section', None, 'tensor'), may hold values from -4 to 4
- wo: bfloat16 [4, 2048, 2048], P('section', 'tensor'), may hold values from -0.125 to 0.125
Outputs:
- section_out: bfloat16 [8, 4, 256, 2048], P('dp', 'section', 'tensor'), parts along dimension 0
- held: bfloat16 [4, 8, 256, 2048], P('section', 'dp', 'tensor'), parts along dimension 1
There are 4 independent parts, one for each index of `dp`. A program takes and returns all parts, laid end to end along the dimension named above; an argument that names none is the same for every part. Nothing has to cross between parts.
All inputs are finite; a program needn't handle non-finite values.
Results may differ from a plain program's by a relative error of at most 0.017.
Values may be sent and summed in bfloat16 or wider, within the bound.
A program may use at most 64 MiB of HBM per device.

v0:
```python
import jax
import jax.numpy as jnp
from jax import lax
from jax.sharding import PartitionSpec as P

HD = 128
TICKS = 2


def from_behind(block, axis, distance):
    devices = range(lax.axis_size(axis))
    route = [(i - distance, i) for i in devices if i - distance in devices]
    return lax.ppermute(block, axis, route)


def normed(rows, gain, bias):
    values = rows.astype(jnp.float32)
    centred = values - jnp.mean(values, axis=-1, keepdims=True)
    spread = jnp.mean(centred * centred, axis=-1, keepdims=True)
    return (centred * lax.rsqrt(spread + 1e-06) * gain + bias).astype(jnp.bfloat16)


def attend(qkv):
    length = qkv.shape[0]
    local_heads = qkv.shape[1] // (3 * HD)
    grid = qkv.reshape(length, local_heads, 3, HD)
    scores = jnp.einsum(
        "qhe,khe->hqk", grid[:, :, 0], grid[:, :, 1], preferred_element_type=jnp.float32
    )
    scores = scores / jnp.sqrt(jnp.float32(HD))
    probs = jax.nn.softmax(scores, axis=-1).astype(jnp.bfloat16)
    mixed = jnp.einsum("hqk,khe->qhe", probs, grid[:, :, 2], preferred_element_type=jnp.float32)
    return mixed.astype(jnp.bfloat16).reshape(length, local_heads * HD)


def body(acts, fresh, order, ln_gain, ln_bias, wqkv, wo):
    gain = ln_gain[0]
    bias = ln_bias[0]
    w_in = wqkv[0]
    w_out = wo[0]
    first = lax.axis_index("section") == 0
    slot_ids = jnp.arange(acts.shape[1], dtype=jnp.int32)
    outputs = []
    slots = acts[0]
    for tick in range(TICKS):
        chosen = order[0, tick]
        current = lax.dynamic_index_in_dim(slots, chosen, 0, keepdims=False)
        qkv = jnp.dot(
            normed(lax.all_gather(current, "tensor", axis=0, tiled=True), gain, bias),
            w_in,
            preferred_element_type=jnp.float32,
        ).astype(jnp.bfloat16)
        mixed = attend(qkv)
        total = lax.psum_scatter(
            jnp.dot(mixed, w_out, preferred_element_type=jnp.float32).astype(jnp.bfloat16),
            "tensor",
            scatter_dimension=0,
            tiled=True,
        ).astype(jnp.float32)
        result = (current.astype(jnp.float32) + total).astype(jnp.bfloat16)
        outputs.append(result)
        arriving = from_behind(result, "section", 1)
        arriving = jnp.where(first, fresh[tick], arriving)
        slots = jnp.where((slot_ids == chosen)[:, None, None], arriving[None], slots)
    return (jnp.stack(outputs, axis=0)[:, None], slots[None])


def solution(mesh):
    return jax.shard_map(
        body,
        mesh=mesh,
        in_specs=(
            P("section", "dp", "tensor", None),
            P("dp", "tensor", None),
            P("section", None),
            P("section", None),
            P("section", None),
            P("section", None, "tensor"),
            P("section", "tensor", None),
        ),
        out_specs=(P("dp", "section", "tensor", None), P("section", "dp", "tensor", None)),
        check_vma=False,
    )
```

profile of v0, /device:TPU:1, one launch (start us, length us, event | category | flops | bytes accessed | tf_op | source)
XLA Modules:
  0.0 174.5 jit_solution(7933763739888886498)
XLA Ops:
  7.2 1.3 fusion.70
  10.5 1.9 %constant_dynamic-slice_fusion = bf16[1,1,128,2048]{3,2,1,0:T(8,128)(2,1)} fusion(bf16[1,2,128,2048]{3,2,1,0:T(8,128)(2,1)} %param.7, s32[]{:T(128)S(6)} %select_n.30), kind=kLoop, calls=%fused_computation.77 | loop fusion | bytes 1048580 | tf_op jit(solution)/shard_map/jit(dynamic_index_in_dim)/dynamic_slice | solution.py:47
  12.4 23.3 %all-gather.5.cloned.1.call-done = bf16[1,1,256,2048]{3,2,1,0:T(8,128)(2,1)} async-done(((bf16[1,1,128,2048]{3,2,1,0:T(8,128)(2,1)}), bf16[1,1,256,2048]{3,2,1,0:T(8,128)(2,1)}) %all-gather.5.cloned.1.call-update) | async-done | bytes 1048592 | tf_op jit(solution)/shard_map/all_gather | solution.py:49
  35.7 1.5 convert_reduce_fusion.1
  37.2 1.6 fusion.25
  38.9 8.2 %fusion.10 = bf16[256,3072]{1,0:T(8,128)(2,1)S(1)} fusion(bf16[1,2048,3072]{2,1,0:T(8,128)(2,1)} %param.12, bf16[1,1,256,2048]{3,2,1,0:T(8,128)(2,1)S(1)} %copy-done.2, f32[2048]{0:T(1024)S(1)} %bitcast.164, f32[2048]{0:T(1024)S(1)} %bitcast.166, f32[256]{0:T(256)S(1)} %add_rsqrt_fusion.1, f32[256]{0:T(256)S(1)} %broadcast_multiply_fusion.1), kind=kOutput, calls=%fused_computation.10 | convolution fusion | flops 3225157632 | bytes 15222784 | tf_op jit(solution)/shard_map/dot_general | solution.py:48
  49.8 4.5 %fusion.16 = bf16[256,2048]{1,0:T(8,128)(2,1)} fusion(bf16[256,1024]{0,1:T(8,128)(2,1)S(1)} %bitcast.168, bf16[1,1024,2048]{2,1,0:T(8,128)(2,1)} %param.13), kind=kOutput, calls=%fused_computation.16 | convolution fusion | flops 1074266112 | bytes 5767168 | tf_op jit(solution)/shard_map/dot_general | solution.py:55
  54.4 20.5 %reduce-scatter.3.cloned.1.call-done = bf16[128,2048]{1,0:T(8,128)(2,1)} async-done(((bf16[256,2048]{1,0:T(8,128)(2,1)}), bf16[128,2048]{1,0:T(8,128)(2,1)}) %reduce-scatter.3.cloned.1.call-update) | async-done | bytes 524304 | tf_op jit(solution)/shard_map/reduce_scatter | solution.py:54
  76.0 3.8 %collective-permute-start = (bf16[128,2048]{1,0:T(8,128)(2,1)S(1)}, bf16[128,2048]{1,0:T(8,128)(2,1)}, u32[]{:S(2)}, u32[]{:S(2)}) collective-permute-start(bf16[128,2048]{1,0:T(8,128)(2,1)S(1)} %fusion.41), channel_id=1, source_target_pairs={{0,8},{8,16},{16,24},{1,9},{9,17},{17,25},{2,10},{10,18},{18,26},{... | collective-permute-start | bytes 1572872 | tf_op jit(solution)/shard_map/ppermute | solution.py:13
  82.8 3.2 %collective-permute-done = bf16[128,2048]{1,0:T(8,128)(2,1)} collective-permute-done((bf16[128,2048]{1,0:T(8,128)(2,1)S(1)}, bf16[128,2048]{1,0:T(8,128)(2,1)}, u32[]{:S(2)}, u32[]{:S(2)}) %collective-permute-start) | collective-permute-done | bytes 524320 | tf_op jit(solution)/shard_map/ppermute | solution.py:13
  87.1 1.5 dynamic-slice_select_fusion
  88.9 21.9 %all-gather.7.cloned.1.call-done = bf16[1,256,2048]{2,1,0:T(8,128)(2,1)} async-done(((bf16[1,128,2048]{2,1,0:T(8,128)(2,1)}), bf16[1,256,2048]{2,1,0:T(8,128)(2,1)}) %all-gather.7.cloned.1.call-update) | async-done | bytes 1048592 | tf_op jit(solution)/shard_map/all_gather | solution.py:49
  110.7 1.5 convert_reduce_fusion
  112.3 1.6 fusion.32
  113.9 9.4 %fusion.13 = bf16[256,3072]{1,0:T(8,128)(2,1)} fusion(bf16[1,2048,3072]{2,1,0:T(8,128)(2,1)} %param.12, bf16[1,256,2048]{2,1,0:T(8,128)(2,1)S(1)} %copy-done.3, f32[256]{0:T(256)S(1)} %add_rsqrt_fusion, f32[256]{0:T(256)S(1)} %broadcast_multiply_fusion, f32[2048]{0:T(1024)S(1)} %bitcast.165, f32[2048]{0:T(1024)S(1)} %bitcast.167), kind=kOutput, calls=%fused_computation.11 | convolution fusion | flops 3225157632 | bytes 15222784 | tf_op jit(solution)/shard_map/dot_general | solution.py:48
  123.4 2.6 %copy.23 = bf16[256,3072]{0,1:T(8,128)(2,1)} copy(bf16[256,3072]{1,0:T(8,128)(2,1)} %fusion.13) | data formatting | bytes 3145728 | tf_op jit(solution)/shard_map/convert_element_type | solution.py:52
  126.0 2.0 %fusion.72 = f32[8,256]{1,0:T(8,128)S(1)} fusion(bf16[256,8,3,128]{0,3,2,1:T(8,128)(2,1)} %bitcast.162), kind=kOutput, calls=%fused_computation.84 | convolution fusion | flops 135790848 | bytes 1056768 | tf_op jit(solution)/shard_map/sub | solution.py:31
  128.0 2.5 %convolution_convert_fusion = bf16[8,128,256]{2,1,0:T(8,128)(2,1)S(1)} fusion(f32[8,256]{1,0:T(8,128)S(1)} %fusion.72, bf16[256,8,3,128]{0,3,2,1:T(8,128)(2,1)} %bitcast.163), kind=kOutput, calls=%fused_computation.40 | convolution fusion | flops 270797056 | bytes 2105344 | tf_op jit(solution)/shard_map/hqk,khe->qhe/dot_general | solution.py:32
  130.5 4.5 %fusion.19 = bf16[256,2048]{1,0:T(8,128)(2,1)} fusion(bf16[256,1024]{0,1:T(8,128)(2,1)S(1)} %bitcast.169, bf16[1,1024,2048]{2,1,0:T(8,128)(2,1)} %param.13), kind=kOutput, calls=%fused_computation.17 | convolution fusion | flops 1074266112 | bytes 5767168 | tf_op jit(solution)/shard_map/dot_general | solution.py:55
  135.0 20.6 %reduce-scatter.5.cloned.1.call-done = bf16[128,2048]{1,0:T(8,128)(2,1)} async-done(((bf16[256,2048]{1,0:T(8,128)(2,1)}), bf16[128,2048]{1,0:T(8,128)(2,1)}) %reduce-scatter.5.cloned.1.call-update) | async-done | bytes 524304 | tf_op jit(solution)/shard_map/reduce_scatter | solution.py:54
  155.6 1.3 fusion.40
  156.8 3.8 %collective-permute-start.1 = (bf16[128,2048]{1,0:T(8,128)(2,1)S(1)}, bf16[128,2048]{1,0:T(8,128)(2,1)S(1)}, u32[]{:S(2)}, u32[]{:S(2)}) collective-permute-start(bf16[128,2048]{1,0:T(8,128)(2,1)S(1)} %fusion.40), channel_id=1, source_target_pairs={{0,8},{8,16},{16,24},{1,9},{9,17},{17,25},{2,10},{10,18},{18,26},{... | collective-permute-start | bytes 1572872 | tf_op jit(solution)/shard_map/ppermute | solution.py:13
  162.3 4.5 %collective-permute-done.1 = bf16[128,2048]{1,0:T(8,128)(2,1)S(1)} collective-permute-done((bf16[128,2048]{1,0:T(8,128)(2,1)S(1)}, bf16[128,2048]{1,0:T(8,128)(2,1)S(1)}, u32[]{:S(2)}, u32[]{:S(2)}) %collective-permute-start.1) | collective-permute-done | bytes 524320 | tf_op jit(solution)/shard_map/ppermute | solution.py:13
  166.8 1.2 select_select_fusion
  (38 shorter events, 8.3 us)
Async XLA Ops:
  7.2 31.7 %copy-start.6 = (f32[1,2048]{1,0:T(1,128)S(1)}, f32[1,2048]{1,0:T(1,128)}, u32[]{:S(2)}) copy-start(f32[1,2048]{1,0:T(1,128)} %param.11) | copy-start | bytes 24580
  7.2 31.7 %copy-start.7 = (f32[1,2048]{1,0:T(1,128)S(1)}, f32[1,2048]{1,0:T(1,128)}, u32[]{:S(2)}) copy-start(f32[1,2048]{1,0:T(1,128)} %param.10) | copy-start | bytes 24580
  7.2 28.5 %all-gather.5.cloned.1.call-start = ((), (), s32[]{:S(2)}) async-start(), calls=%async_computation.4 | async-start | bytes 1572864 | tf_op jit(solution)/shard_map/all_gather | solution.py:49
  12.4 62.5 %reduce-scatter.3.cloned.1.call-start = ((), (), s32[]{:S(2)}) async-start(), calls=%async_computation.2 | async-start | bytes 1572864 | tf_op jit(solution)/shard_map/reduce_scatter | solution.py:54
  35.7 3.2 %copy-start.2 = (bf16[1,1,256,2048]{3,2,1,0:T(8,128)(2,1)S(1)}, bf16[1,1,256,2048]{3,2,1,0:T(8,128)(2,1)}, u32[]{:S(2)}) copy-start(bf16[1,1,256,2048]{3,2,1,0:T(8,128)(2,1)} %all-gather.5.cloned.1.call-done) | copy-start | bytes 3145732
  49.8 25.1 %copy-start = (bf16[1,2,128,2048]{3,2,1,0:T(8,128)(2,1)S(1)}, bf16[1,2,128,2048]{3,2,1,0:T(8,128)(2,1)}, u32[]{:S(2)}) copy-start(bf16[1,2,128,2048]{3,2,1,0:T(8,128)(2,1)} %param.7) | copy-start | bytes 3145732
  54.3 31.7 %copy-start.4 = (bf16[2,128,2048]{2,1,0:T(8,128)(2,1)S(1)}, bf16[2,128,2048]{2,1,0:T(8,128)(2,1)}, u32[]{:S(2)}) copy-start(bf16[2,128,2048]{2,1,0:T(8,128)(2,1)} %param.8) | copy-start | bytes 3145732
  54.3 56.4 %all-gather.7.cloned.1.call-start = ((), (), s32[]{:S(2)}) async-start(), calls=%async_computation.5 | async-start | bytes 1572864 | tf_op jit(solution)/shard_map/all_gather | solution.py:49
  76.0 10.0 %collective-permute-start = (bf16[128,2048]{1,0:T(8,128)(2,1)S(1)}, bf16[128,2048]{1,0:T(8,128)(2,1)}, u32[]{:S(2)}, u32[]{:S(2)}) collective-permute-start(bf16[128,2048]{1,0:T(8,128)(2,1)S(1)} %fusion.41), channel_id=1, source_target_pairs={{0,8},{8,16},{16,24},{1,9},{9,17},{17,25},{2,10},{10,18},{18,26},{... | collective-permute-start | bytes 1572872 | tf_op jit(solution)/shard_map/ppermute | solution.py:13
  88.6 66.9 %reduce-scatter.5.cloned.1.call-start = ((), (), s32[]{:S(2)}) async-start(), calls=%async_computation.3 | async-start | bytes 1572864 | tf_op jit(solution)/shard_map/reduce_scatter | solution.py:54
  110.7 3.2 %copy-start.3 = (bf16[1,256,2048]{2,1,0:T(8,128)(2,1)S(1)}, bf16[1,256,2048]{2,1,0:T(8,128)(2,1)}, u32[]{:S(2)}) copy-start(bf16[1,256,2048]{2,1,0:T(8,128)(2,1)} %all-gather.7.cloned.1.call-done) | copy-start | bytes 3145732
  130.5 25.1 %copy-start.1 = (bf16[1,128,2048]{2,1,0:T(8,128)(2,1)S(1)}, bf16[1,128,2048]{2,1,0:T(8,128)(2,1)}, u32[]{:S(2)}) copy-start(bf16[1,128,2048]{2,1,0:T(8,128)(2,1)} %dynamic-slice_select_fusion) | copy-start | bytes 1572868
  155.6 11.2 %copy-start.5 = (bf16[2,128,2048]{2,1,0:T(8,128)(2,1)S(1)}, bf16[2,128,2048]{2,1,0:T(8,128)(2,1)}, u32[]{:S(2)}) copy-start(bf16[2,128,2048]{2,1,0:T(8,128)(2,1)} %param.8) | copy-start | bytes 3145732
  156.8 9.9 %collective-permute-start.1 = (bf16[128,2048]{1,0:T(8,128)(2,1)S(1)}, bf16[128,2048]{1,0:T(8,128)(2,1)S(1)}, u32[]{:S(2)}, u32[]{:S(2)}) collective-permute-start(bf16[128,2048]{1,0:T(8,128)(2,1)S(1)} %fusion.40), channel_id=1, source_target_pairs={{0,8},{8,16},{16,24},{1,9},{9,17},{17,25},{2,10},{10,18},{18,26},{... | collective-permute-start | bytes 1572872 | tf_op jit(solution)/shard_map/ppermute | solution.py:13
Sparse Core Ops, SparseCore 0:
  12.5 23.1 all-gather.4
  54.5 20.3 reduce-scatter.2
  88.8 21.9 all-gather.6
  135.1 20.3 reduce-scatter.4
where the time goes:
time: 175 us
  waiting for transfers between devices  94 us (54%)
  matrix products  33.1 us (19%)
  between operations  17.5 us (10%)
  other arithmetic  14.9 us (9%)
  starting transfers between devices  8 us (5%)
  local copies, waits for them, and re-layouts  7.08 us (4%)
    all_gather x2, waiting for transfers between devices, body(): lax.all_gather(current, 'tensor', axis=0, tiled=True)  45.1 us
    reduce_scatter x2, waiting for transfers between devices, body(): lax.psum_scatter(jnp.dot(mixed, w_out, preferred_element_type=jnp.float32...  41 us
    dot_general x2, matrix products, body(): jnp.dot(normed(lax.all_gather(current, 'tensor', axis=0, tiled=True), gai...  17.6 us
    dot_general x2, matrix products, body(): jnp.dot(mixed, w_out, preferred_element_type=jnp.float32)  9 us
    ppermute x2, waiting for transfers between devices, from_behind(): return lax.ppermute(block, axis, route)  7.71 us
    ppermute x2, starting transfers between devices, from_behind(): return lax.ppermute(block, axis, route)  7.66 us
    dot_general x2, matrix products, attend(): jnp.einsum('hqk,khe->qhe', probs, grid[:, :, 2], preferred_element_type=j...  3.6 us
  transfers between devices with their start and end apart: 6, of which 6 were waited for; matrix products, arithmetic and copies ran while one was open for 2% of the time, Pallas kernels for 0%

commit v1 on v0

v1 whole, which is shorter than its diff:
```python
import functools
import math

import jax
import jax.numpy as jnp
from jax import lax
from jax.experimental import pallas as pl
from jax.experimental.pallas import tpu as pltpu
from jax.sharding import PartitionSpec as P

HD = 128
EPS = 1e-06
CHUNK = 32
BLOCK = 64
TILE = 512
PIECE = 16
MESH = pl.DeviceIdType.MESH


def relay(
    acts, fresh, order, gain, bias, w_in, w_out, out, held,
    slots, fresh_v, wi, wo, xs, h, qkv, mixed, part, got, res, arr,
    load_sem, wi_sem, wo_sem, out_sem, held_sem,
    ag_send, ag_recv, rs_send, rs_recv, hop_send, hop_recv,
):
    ticks, rows, width = fresh.shape
    n_slots = acts.shape[1]
    peers = lax.axis_size("tensor")
    sections = lax.axis_size("section")
    me = lax.axis_index("tensor")
    sec = lax.axis_index("section")
    seq = rows * peers
    heads = wi.shape[1] // (3 * HD)
    block = min(BLOCK, rows)
    chunk = min(CHUNK, block)
    n_chunks = rows // chunk
    n_blocks = rows // block
    per_block = block // chunk
    wi_tile = min(TILE, wi.shape[1])
    wo_tile = min(TILE, width)
    has_prev = sec > 0
    has_next = sec < sections - 1

    load_acts = pltpu.make_async_copy(acts.at[0], slots, load_sem.at[0])
    load_acts.start()

    def wi_copy(i):
        cols = pl.ds(pl.multiple_of(i * wi_tile, wi_tile), wi_tile)
        return pltpu.make_async_copy(w_in.at[0, :, cols], wi.at[:, cols], wi_sem.at[i])

    for i in range(wi.shape[1] // wi_tile):
        wi_copy(i).start()
    load_wo = pltpu.make_async_copy(w_out.at[0], wo, wo_sem)
    load_wo.start()
    load_fresh = pltpu.make_async_copy(fresh, fresh_v, load_sem.at[1])
    load_fresh.start()

    barrier = pltpu.get_barrier_semaphore()
    for d in range(1, peers):
        pl.semaphore_signal(
            barrier, inc=1, device_id={"tensor": lax.rem(me + d, peers)}, device_id_type=MESH
        )

    @pl.when(has_prev)
    def _():
        pl.semaphore_signal(barrier, inc=1, device_id={"section": sec - 1}, device_id_type=MESH)

    @pl.when(has_next)
    def _():
        pl.semaphore_signal(barrier, inc=1, device_id={"section": sec + 1}, device_id_type=MESH)

    def ag_copy(t, d, c):
        return pltpu.make_async_remote_copy(
            src_ref=xs.at[t, 0, pl.ds(c * chunk, chunk)],
            dst_ref=xs.at[t, d, pl.ds(c * chunk, chunk)],
            send_sem=ag_send.at[t, d - 1, c],
            recv_sem=ag_recv.at[t, d - 1, c],
            device_id={"tensor": lax.rem(me + d, peers)},
            device_id_type=MESH,
        )

    def rs_copy(t, d, c):
        return pltpu.make_async_remote_copy(
            src_ref=part.at[t, d, pl.ds(c * chunk, chunk)],
            dst_ref=got.at[t, d - 1, pl.ds(c * chunk, chunk)],
            send_sem=rs_send.at[t, d - 1, c],
            recv_sem=rs_recv.at[t, d - 1, c],
            device_id={"tensor": lax.rem(me - d + peers, peers)},
            device_id_type=MESH,
        )

    def hop_copy(t, c):
        return pltpu.make_async_remote_copy(
            src_ref=res.at[t, pl.ds(c * chunk, chunk)],
            dst_ref=arr.at[t, pl.ds(c * chunk, chunk)],
            send_sem=hop_send.at[t, c],
            recv_sem=hop_recv.at[t, c],
            device_id={"section": lax.rem(sec + 1, sections)},
            device_id_type=MESH,
        )

    def pieces(start, count, step):
        def one(i, carry):
            step(pl.ds(pl.multiple_of(start + i * PIECE, PIECE), PIECE))
            return carry

        lax.fori_loop(0, count // PIECE, one, 0)

    def offer(t, c):
        chosen = order[0, t]

        def step(r):
            xs[t, 0, r, :] = slots[chosen, r, :]

        pieces(c * chunk, chunk, step)

    def send_offer(t, c):
        for d in range(1, peers):
            ag_copy(t, d, c).start()

    def norm(t, d, start, count):
        g = gain[0:1, :]
        b = bias[0:1, :]

        def step(r):
            values = xs[t, d, r, :].astype(jnp.float32)
            centred = values - jnp.mean(values, axis=-1, keepdims=True)
            spread = jnp.mean(centred * centred, axis=-1, keepdims=True)
            h[r, :] = (centred * lax.rsqrt(spread + EPS) * g + b).astype(jnp.bfloat16)

        pieces(start, count, step)

    def project(d, start, count, first):
        def one(i, carry):
            if first:
                wi_copy(i).wait()
            cols = pl.ds(pl.multiple_of(i * wi_tile, wi_tile), wi_tile)
            y = jnp.dot(h[pl.ds(start, count), :], wi[:, cols], preferred_element_type=jnp.float32)
            qkv[pl.ds(d * rows + start, count), cols] = y.astype(jnp.bfloat16)
            return carry

        lax.fori_loop(0, wi.shape[1] // wi_tile, one, 0)

    scale = math.log2(math.e) / math.sqrt(HD)

    def attend(t, d, b):
        r = pl.ds(pl.multiple_of(d * rows + b * block, block), block)
        for n in range(heads):
            base = n * 3 * HD
            q = qkv[r, base:base + HD]
            k = qkv[:, base + HD:base + 2 * HD]
            v = qkv[:, base + 2 * HD:base + 3 * HD]
            s = lax.dot_general(q, k, (((1,), (1,)), ((), ())), preferred_element_type=jnp.float32)
            e = jnp.exp2((s - jnp.max(s, axis=-1, keepdims=True)) * scale)
            total = jnp.sum(e, axis=-1, keepdims=True)
            y = jnp.dot(e.astype(jnp.bfloat16), v, preferred_element_type=jnp.float32)
            mixed[:, n * HD:(n + 1) * HD] = (y / total).astype(jnp.bfloat16)

        def one(i, carry):
            cols = pl.ds(pl.multiple_of(i * wo_tile, wo_tile), wo_tile)
            y = jnp.dot(mixed[...], wo[:, cols], preferred_element_type=jnp.float32)
            part[t, d, pl.ds(pl.multiple_of(b * block, block), block), cols] = y.astype(jnp.bfloat16)
            return carry

        lax.fori_loop(0, width // wo_tile, one, 0)

    def finish(t, c):
        for d in range(1, peers):
            rs_copy(t, d, c).wait_recv()

        def step(r):
            total = part[t, 0, r, :].astype(jnp.float32)
            for d in range(1, peers):
                total = total + got[t, d - 1, r, :].astype(jnp.float32)
            res[t, r, :] = (xs[t, 0, r, :].astype(jnp.float32) + total).astype(jnp.bfloat16)

        pieces(c * chunk, chunk, step)

        @pl.when(has_next)
        def _():
            hop_copy(t, c).start()

    def take(t, c):
        chosen = order[0, t]

        @pl.when(has_prev)
        def _():
            hop_copy(t, c).wait_recv()

        def step(r, source):
            new = source[t, r, :].astype(jnp.float32)
            for k in range(n_slots):
                old = slots[k, r, :].astype(jnp.float32)
                slots[k, r, :] = jnp.where(chosen == k, new, old).astype(jnp.bfloat16)

        @pl.when(has_prev)
        def _():
            pieces(c * chunk, chunk, functools.partial(step, source=arr))

        @pl.when(jnp.logical_not(has_prev))
        def _():
            pieces(c * chunk, chunk, functools.partial(step, source=fresh_v))

    def held_copy(c):
        r = pl.ds(c * chunk, chunk)
        return pltpu.make_async_copy(slots.at[:, r], held.at[0, :, r], held_sem.at[c])

    def out_copy(t):
        return pltpu.make_async_copy(res.at[t], out.at[t, 0], out_sem.at[t])

    load_acts.wait()
    for c in range(n_chunks):
        offer(0, c)
    pl.semaphore_wait(
        barrier, peers - 1 + has_prev.astype(jnp.int32) + has_next.astype(jnp.int32)
    )
    for c in range(n_chunks):
        send_offer(0, c)

    for t in range(ticks):
        norm(t, 0, 0, rows)
        project(0, 0, rows, t == 0)
        for b in range(n_blocks):
            for d in range(1, peers):
                for c in range(b * per_block, (b + 1) * per_block):
                    ag_copy(t, d, c).wait_recv()
                norm(t, d, b * block, block)
                project(d, b * block, block, False)
        if t == 0:
            load_wo.wait()
        for d in [*range(1, peers), 0]:
            def blocks(b, carry, d=d):
                attend(t, d, b)
                if d:
                    for c in range(per_block):
                        rs_copy(t, d, b * per_block + c).start()
                return carry

            lax.fori_loop(0, n_blocks, blocks, 0)
        if t == 0:
            load_fresh.wait()
        lag = 1
        for step in range(n_chunks + lag):
            if step < n_chunks:
                finish(t, step)
            if step == n_chunks - 1:
                out_copy(t).start()
            if step >= lag:
                take(t, step - lag)
                if t + 1 < ticks:
                    offer(t + 1, step - lag)
                    send_offer(t + 1, step - lag)
                else:
                    held_copy(step - lag).start()

    for t in range(ticks):
        for c in range(n_chunks):
            for d in range(1, peers):
                ag_copy(t, d, c).wait_send()
                rs_copy(t, d, c).wait_send()

            @pl.when(has_next)
            def _():
                hop_copy(t, c).wait_send()

        out_copy(t).wait()
    for c in range(n_chunks):
        held_copy(c).wait()


def body(acts, fresh, order, ln_gain, ln_bias, wqkv, wo):
    ticks, rows, width = fresh.shape
    n_slots = acts.shape[1]
    peers = lax.axis_size("tensor")
    seq = rows * peers
    block = min(BLOCK, rows)
    n_chunks = rows // min(CHUNK, block)
    inner = wo.shape[1]
    wide = wqkv.shape[2]
    bf = jnp.bfloat16
    dma = pltpu.SemaphoreType.DMA
    anywhere = pl.BlockSpec(memory_space=pl.ANY)
    vmem = pl.BlockSpec(memory_space=pltpu.VMEM)
    smem = pl.BlockSpec(memory_space=pltpu.SMEM)
    return pl.pallas_call(
        relay,
        out_shape=(
            jax.ShapeDtypeStruct((ticks, 1, rows, width), bf),
            jax.ShapeDtypeStruct((1, n_slots, rows, width), bf),
        ),
        in_specs=[anywhere, anywhere, smem, vmem, vmem, anywhere, anywhere],
        out_specs=(anywhere, anywhere),
        scratch_shapes=[
            pltpu.VMEM((n_slots, rows, width), bf),
            pltpu.VMEM((ticks, rows, width), bf),
            pltpu.VMEM((width, wide), bf),
            pltpu.VMEM((inner, width), bf),
            pltpu.VMEM((ticks, peers, rows, width), bf),
            pltpu.VMEM((rows, width), bf),
            pltpu.VMEM((seq, wide), bf),
            pltpu.VMEM((block, inner), bf),
            pltpu.VMEM((ticks, peers, rows, width), bf),
            pltpu.VMEM((ticks, peers - 1, rows, width), bf),
            pltpu.VMEM((ticks, rows, width), bf),
            pltpu.VMEM((ticks, rows, width), bf),
            dma((2,)),
            dma((wide // min(TILE, wide),)),
            dma,
            dma((ticks,)),
            dma((n_chunks,)),
            dma((ticks, peers - 1, n_chunks)),
            dma((ticks, peers - 1, n_chunks)),
            dma((ticks, peers - 1, n_chunks)),
            dma((ticks, peers - 1, n_chunks)),
            dma((ticks, n_chunks)),
            dma((ticks, n_chunks)),
        ],
        compiler_params=pltpu.CompilerParams(
            collective_id=0, has_side_effects=True, vmem_limit_bytes=60 * 1024 * 1024
        ),
    )(acts, fresh, order, ln_gain, ln_bias, wqkv, wo)


def solution(mesh):
    return jax.shard_map(
        body,
        mesh=mesh,
        in_specs=(
            P("section", "dp", "tensor", None),
            P("dp", "tensor", None),
            P("section", None),
            P("section", None),
            P("section", None),
            P("section", None, "tensor"),
            P("section", "tensor", None),
        ),
        out_specs=(P("dp", "section", "tensor", None), P("section", "dp", "tensor", None)),
        check_vma=False,
    )
```

time: 175 us -> 78.6 us (0.45)
  waiting for transfers between devices: 94 us -> 0 us
  Pallas kernels: 0 us -> 72.5 us
  matrix products: 33.1 us -> 0 us
  between operations: 17.5 us -> 0.64 us
  other arithmetic: 14.9 us -> 0 us
  starting transfers between devices: 8 us -> 0 us
  local copies, waits for them, and re-layouts: 7.08 us -> 4.61 us
    pallas_call x0 -> x1, Pallas kernels: none -> 72.5 us  [body(): pl.pallas_call(relay, out_shape=(jax.ShapeDtypeStruct((ticks, 1, rows, wi...]
    all_gather x2 -> x0, waiting for transfers between devices: 45.1 us -> none  [body(): lax.all_gather(current, 'tensor', axis=0, tiled=True)]
    reduce_scatter x2 -> x0, waiting for transfers between devices: 41 us -> none  [body(): lax.psum_scatter(jnp.dot(mixed, w_out, preferred_element_type=jnp.float32...]
    dot_general x6 -> x0, matrix products: 30.2 us -> none  [the longest x2 17.6 us: body(): jnp.dot(normed(lax.all_gather(current, 'tensor', axis=0, tiled=True), gai...]
    ppermute x2 -> x0, waiting for transfers between devices: 7.71 us -> none  [from_behind(): return lax.ppermute(block, axis, route)]
    ppermute x2 -> x0, starting transfers between devices: 7.66 us -> none  [from_behind(): return lax.ppermute(block, axis, route)]
    reduce_sum x4 -> x0, other arithmetic: 6.34 us -> none  [the longest x2 3.28 us: normed(): spread = jnp.mean(centred * centred, axis=-1, keepdims=True)]
    unnamed x16 -> x2, local copies, waits for them, and re-layouts: 0.04 us -> 4.61 us
  transfers between devices with their start and end apart: 6 -> 0, of which waited for: 6 -> 0; matrix products, arithmetic and copies ran while one was open for 2% -> 0% of each run, Pallas kernels for 0% -> 0%
where the time goes in v1:
time: 78.6 us; the launch traced here: 77.7 us
  Pallas kernels  72.5 us (92%)
  local copies, waits for them, and re-layouts  4.61 us (6%)
    pallas_call x1, Pallas kernels, body(): pl.pallas_call(relay, out_shape=(jax.ShapeDtypeStruct((ticks, 1, rows, wi...  72.5 us
    unnamed x2, local copies, waits for them, and re-layouts  4.61 us

profile of v1, /device:TPU:1, one launch (start us, length us, event | category | flops | bytes accessed | tf_op | source)
XLA Modules:
  0.0 77.7 jit_solution(5346879492827700072)
XLA Ops:
  0.6 72.5 %shard_map.86 = (bf16[2,1,128,2048]{3,2,1,0:T(8,128)(2,1)}, bf16[1,2,128,2048]{3,2,1,0:T(8,128)(2,1)}) custom-call(bf16[1,2,128,2048]{3,2,1,0:T(8,128)(2,1)} %acts.1, bf16[2,128,2048]{2,1,0:T(8,128)(2,1)} %fresh.1, s32[1,2]{1,0:T(1,128)} %order.1, f32[1,2048]{1,0:T(1,128)} %gain.1, f32[1,2048]{1,0:T(1,128)} %bias.1, bf16[1,2048,3072]{2,1,0:T(8,128)(2,1)} %w_in.1, ...), custom_call_target="tpu_custom_call" | custom-call | tf_op jit(solution)/shard_map/pallas_call | solution.py:285
  73.1 2.3 %copy.11 = bf16[2,1,128,2048]{3,2,1,0:T(8,128)(2,1)} copy(bf16[2,1,128,2048]{3,2,1,0:T(8,128)(2,1)} %get-tuple-element.4) | data formatting | bytes 2097152
  75.4 2.3 %copy.12 = bf16[1,2,128,2048]{3,2,1,0:T(8,128)(2,1)} copy(bf16[1,2,128,2048]{3,2,1,0:T(8,128)(2,1)} %get-tuple-element.5) | data formatting | bytes 2097152

commit v2 on v1

v2 whole, which is shorter than its diff:
```python
import functools
import math

import jax
import jax.numpy as jnp
from jax import lax
from jax.experimental import pallas as pl
from jax.experimental.pallas import tpu as pltpu
from jax.sharding import PartitionSpec as P

HD = 128
EPS = 1e-06
CHUNK = 512
TILE = 1024
NORM_ROWS = 16
PIECE = 32
MESH = pl.DeviceIdType.MESH


def fitting(most, size):
    return math.gcd(most, size)


def relay(
    acts, fresh, order, gain, bias, w_in, w_out, out, held,
    slots, fresh_v, wi, wo, xs, h, qkv, mixed, part, got, res, arr,
    acts_sem, fresh_sem, wi_sem, wo_sem, out_sem, held_sem,
    ag_send, ag_recv, rs_send, rs_recv, hop_send, hop_recv,
):
    ticks, rows, width = fresh.shape
    n_slots = acts.shape[1]
    peers = lax.axis_size("tensor")
    sections = lax.axis_size("section")
    me = lax.axis_index("tensor")
    sec = lax.axis_index("section")
    seq = rows * peers
    heads = wi.shape[1] // (3 * HD)
    chunk = fitting(CHUNK, width)
    n_chunks = width // chunk
    wi_tile = fitting(TILE, wi.shape[1])
    n_tiles = wi.shape[1] // wi_tile
    has_prev = sec > 0
    has_next = sec < sections - 1

    def span(c):
        return pl.ds(c * chunk, chunk)

    def acts_copy(c):
        return pltpu.make_async_copy(acts.at[0, :, :, span(c)], slots.at[:, :, span(c)], acts_sem.at[c])

    for c in range(n_chunks):
        acts_copy(c).start()

    def wi_copy(i):
        cols = pl.ds(i * wi_tile, wi_tile)
        return pltpu.make_async_copy(w_in.at[0, :, cols], wi.at[:, cols], wi_sem.at[i])

    for i in range(n_tiles):
        wi_copy(i).start()
    load_wo = pltpu.make_async_copy(w_out.at[0], wo, wo_sem)
    load_wo.start()
    load_fresh = pltpu.make_async_copy(fresh, fresh_v, fresh_sem)
    load_fresh.start()

    barrier = pltpu.get_barrier_semaphore()
    for d in range(1, peers):
        pl.semaphore_signal(
            barrier, inc=1, device_id={"tensor": lax.rem(me + d, peers)}, device_id_type=MESH
        )

    @pl.when(has_prev)
    def _():
        pl.semaphore_signal(barrier, inc=1, device_id={"section": sec - 1}, device_id_type=MESH)

    @pl.when(has_next)
    def _():
        pl.semaphore_signal(barrier, inc=1, device_id={"section": sec + 1}, device_id_type=MESH)

    def ag_copy(t, d, c):
        return pltpu.make_async_remote_copy(
            src_ref=xs.at[t, 0, :, span(c)],
            dst_ref=xs.at[t, d, :, span(c)],
            send_sem=ag_send.at[t, d - 1, c],
            recv_sem=ag_recv.at[t, d - 1, c],
            device_id={"tensor": lax.rem(me + d, peers)},
            device_id_type=MESH,
        )

    def rs_copy(t, d, c):
        return pltpu.make_async_remote_copy(
            src_ref=part.at[t, d, :, span(c)],
            dst_ref=got.at[t, d - 1, :, span(c)],
            send_sem=rs_send.at[t, d - 1, c],
            recv_sem=rs_recv.at[t, d - 1, c],
            device_id={"tensor": lax.rem(me - d + peers, peers)},
            device_id_type=MESH,
        )

    def hop_copy(t, c):
        return pltpu.make_async_remote_copy(
            src_ref=res.at[t, :, span(c)],
            dst_ref=arr.at[t, :, span(c)],
            send_sem=hop_send.at[t, c],
            recv_sem=hop_recv.at[t, c],
            device_id={"section": lax.rem(sec + 1, sections)},
            device_id_type=MESH,
        )

    def pieces(step):
        for i in range(rows // PIECE):
            step(pl.ds(i * PIECE, PIECE))

    def offer(t, c):
        chosen = order[0, t]

        def step(r):
            x = slots[0, r, span(c)].astype(jnp.float32)
            for k in range(1, n_slots):
                x = jnp.where(chosen == k, slots[k, r, span(c)].astype(jnp.float32), x)
            xs[t, 0, r, span(c)] = x.astype(jnp.bfloat16)

        pieces(step)

    def send_offer(t, c):
        for d in range(1, peers):
            ag_copy(t, d, c).start()

    def norm(t, d):
        g = gain[0:1, :]
        b = bias[0:1, :]

        def one(i, carry):
            r = pl.ds(pl.multiple_of(i * NORM_ROWS, NORM_ROWS), NORM_ROWS)
            values = xs[t, d, r, :].astype(jnp.float32)
            centred = values - jnp.mean(values, axis=-1, keepdims=True)
            spread = jnp.mean(centred * centred, axis=-1, keepdims=True)
            h[r, :] = (centred * lax.rsqrt(spread + EPS) * g + b).astype(jnp.bfloat16)
            return carry

        lax.fori_loop(0, rows // NORM_ROWS, one, 0, unroll=2)

    def project(d, first):
        for i in range(n_tiles):
            if first:
                wi_copy(i).wait()
            cols = pl.ds(i * wi_tile, wi_tile)
            y = jnp.dot(h[...], wi[:, cols], preferred_element_type=jnp.float32)
            qkv[d * rows:(d + 1) * rows, cols] = y.astype(jnp.bfloat16)

    scale = math.log2(math.e) / math.sqrt(HD)

    def attend(t, d):
        r = slice(d * rows, (d + 1) * rows)
        for n in range(heads):
            base = n * 3 * HD
            q = qkv[r, base:base + HD]
            k = qkv[:, base + HD:base + 2 * HD]
            v = qkv[:, base + 2 * HD:base + 3 * HD]
            s = lax.dot_general(q, k, (((1,), (1,)), ((), ())), preferred_element_type=jnp.float32)
            e = jnp.exp2((s - jnp.max(s, axis=-1, keepdims=True)) * scale)
            total = jnp.sum(e, axis=-1, keepdims=True)
            y = jnp.dot(e.astype(jnp.bfloat16), v, preferred_element_type=jnp.float32)
            mixed[:, n * HD:(n + 1) * HD] = (y / total).astype(jnp.bfloat16)

        for c in range(n_chunks):
            y = jnp.dot(mixed[...], wo[:, span(c)], preferred_element_type=jnp.float32)
            part[t, d, :, span(c)] = y.astype(jnp.bfloat16)
            if d:
                rs_copy(t, d, c).start()

    def finish(t, c):
        for d in range(1, peers):
            rs_copy(t, d, c).wait_recv()

        def step(r):
            total = part[t, 0, r, span(c)].astype(jnp.float32)
            for d in range(1, peers):
                total = total + got[t, d - 1, r, span(c)].astype(jnp.float32)
            x = xs[t, 0, r, span(c)].astype(jnp.float32)
            res[t, r, span(c)] = (x + total).astype(jnp.bfloat16)

        pieces(step)

        @pl.when(has_next)
        def _():
            hop_copy(t, c).start()

    def take(t, c):
        chosen = order[0, t]

        @pl.when(has_prev)
        def _():
            hop_copy(t, c).wait_recv()

        def step(r, source):
            new = source[t, r, span(c)].astype(jnp.float32)
            for k in range(n_slots):
                old = slots[k, r, span(c)].astype(jnp.float32)
                slots[k, r, span(c)] = jnp.where(chosen == k, new, old).astype(jnp.bfloat16)

        @pl.when(has_prev)
        def _():
            pieces(functools.partial(step, source=arr))

        @pl.when(jnp.logical_not(has_prev))
        def _():
            pieces(functools.partial(step, source=fresh_v))

    def held_copy(c):
        return pltpu.make_async_copy(slots.at[:, :, span(c)], held.at[0, :, :, span(c)], held_sem.at[c])

    def out_copy(t):
        return pltpu.make_async_copy(res.at[t], out.at[t, 0], out_sem.at[t])

    for c in range(n_chunks):
        acts_copy(c).wait()
        offer(0, c)
    pl.semaphore_wait(
        barrier, peers - 1 + has_prev.astype(jnp.int32) + has_next.astype(jnp.int32)
    )
    for c in range(n_chunks):
        send_offer(0, c)

    for t in range(ticks):
        norm(t, 0)
        project(0, t == 0)
        for d in range(1, peers):
            for c in range(n_chunks):
                ag_copy(t, d, c).wait_recv()
            norm(t, d)
            project(d, False)
        if t == 0:
            load_wo.wait()
        for d in [*range(1, peers), 0]:
            attend(t, d)
        if t == 0:
            load_fresh.wait()
        lag = 1
        for step in range(n_chunks + lag):
            if step < n_chunks:
                finish(t, step)
            if step == n_chunks - 1:
                out_copy(t).start()
            if step >= lag:
                take(t, step - lag)
                if t + 1 < ticks:
                    offer(t + 1, step - lag)
                    send_offer(t + 1, step - lag)
                else:
                    held_copy(step - lag).start()

    for t in range(ticks):
        for c in range(n_chunks):
            for d in range(1, peers):
                ag_copy(t, d, c).wait_send()
                rs_copy(t, d, c).wait_send()

            @pl.when(has_next)
            def _():
                hop_copy(t, c).wait_send()

        out_copy(t).wait()
    for c in range(n_chunks):
        held_copy(c).wait()


def body(acts, fresh, order, ln_gain, ln_bias, wqkv, wo):
    ticks, rows, width = fresh.shape
    n_slots = acts.shape[1]
    peers = lax.axis_size("tensor")
    seq = rows * peers
    n_chunks = width // fitting(CHUNK, width)
    inner = wo.shape[1]
    wide = wqkv.shape[2]
    bf = jnp.bfloat16
    dma = pltpu.SemaphoreType.DMA
    anywhere = pl.BlockSpec(memory_space=pl.ANY)
    vmem = pl.BlockSpec(memory_space=pltpu.VMEM)
    smem = pl.BlockSpec(memory_space=pltpu.SMEM)
    return pl.pallas_call(
        relay,
        out_shape=(
            jax.ShapeDtypeStruct((ticks, 1, rows, width), bf),
            jax.ShapeDtypeStruct((1, n_slots, rows, width), bf),
        ),
        in_specs=[anywhere, anywhere, smem, vmem, vmem, anywhere, anywhere],
        out_specs=(anywhere, anywhere),
        scratch_shapes=[
            pltpu.VMEM((n_slots, rows, width), bf),
            pltpu.VMEM((ticks, rows, width), bf),
            pltpu.VMEM((width, wide), bf),
            pltpu.VMEM((inner, width), bf),
            pltpu.VMEM((ticks, peers, rows, width), bf),
            pltpu.VMEM((rows, width), bf),
            pltpu.VMEM((seq, wide), bf),
            pltpu.VMEM((rows, inner), bf),
            pltpu.VMEM((ticks, peers, rows, width), bf),
            pltpu.VMEM((ticks, peers - 1, rows, width), bf),
            pltpu.VMEM((ticks, rows, width), bf),
            pltpu.VMEM((ticks, rows, width), bf),
            dma((n_chunks,)),
            dma,
            dma((wide // fitting(TILE, wide),)),
            dma,
            dma((ticks,)),
            dma((n_chunks,)),
            dma((ticks, peers - 1, n_chunks)),
            dma((ticks, peers - 1, n_chunks)),
            dma((ticks, peers - 1, n_chunks)),
            dma((ticks, peers - 1, n_chunks)),
            dma((ticks, n_chunks)),
            dma((ticks, n_chunks)),
        ],
        compiler_params=pltpu.CompilerParams(
            collective_id=0, has_side_effects=True, vmem_limit_bytes=60 * 1024 * 1024
        ),
    )(acts, fresh, order, ln_gain, ln_bias, wqkv, wo)


def solution(mesh):
    return jax.shard_map(
        body,
        mesh=mesh,
        in_specs=(
            P("section", "dp", "tensor", None),
            P("dp", "tensor", None),
            P("section", None),
            P("section", None),
            P("section", None),
            P("section", None, "tensor"),
            P("section", "tensor", None),
        ),
        out_specs=(P("dp", "section", "tensor", None), P("section", "dp", "tensor", None)),
        check_vma=False,
    )
```

time: 78.6 us -> 69.4 us (0.88)
  Pallas kernels: 72.5 us -> 64 us
    pallas_call x1, Pallas kernels: 72.5 us -> 64 us  [body(): pl.pallas_call(relay, out_shape=(jax.ShapeDtypeStruct((ticks, 1, rows, wi...]
where the time goes in v2:
time: 69.4 us; the launch traced here: 69.2 us
  Pallas kernels  64 us (92%)
  local copies, waits for them, and re-layouts  4.61 us (7%)
    pallas_call x1, Pallas kernels, body(): pl.pallas_call(relay, out_shape=(jax.ShapeDtypeStruct((ticks, 1, rows, wi...  64 us
    unnamed x2, local copies, waits for them, and re-layouts  4.61 us

profile of v2, /device:TPU:1, one launch (start us, length us, event | category | flops | bytes accessed | tf_op | source)
XLA Modules:
  0.0 69.2 jit_solution(7702281364789575113)
XLA Ops:
  0.6 64.0 %shard_map.86 = (bf16[2,1,128,2048]{3,2,1,0:T(8,128)(2,1)}, bf16[1,2,128,2048]{3,2,1,0:T(8,128)(2,1)}) custom-call(bf16[1,2,128,2048]{3,2,1,0:T(8,128)(2,1)} %acts.1, bf16[2,128,2048]{2,1,0:T(8,128)(2,1)} %fresh.1, s32[1,2]{1,0:T(1,128)} %order.1, f32[1,2048]{1,0:T(1,128)} %gain.1, f32[1,2048]{1,0:T(1,128)} %bias.1, bf16[1,2048,3072]{2,1,0:T(8,128)(2,1)} %w_in.1, ...), custom_call_target="tpu_custom_call" | custom-call | tf_op jit(solution)/shard_map/pallas_call | solution.py:280
  64.6 2.3 %copy.11 = bf16[2,1,128,2048]{3,2,1,0:T(8,128)(2,1)} copy(bf16[2,1,128,2048]{3,2,1,0:T(8,128)(2,1)} %get-tuple-element.4) | data formatting | bytes 2097152
  66.9 2.3 %copy.12 = bf16[1,2,128,2048]{3,2,1,0:T(8,128)(2,1)} copy(bf16[1,2,128,2048]{3,2,1,0:T(8,128)(2,1)} %get-tuple-element.5) | data formatting | bytes 2097152

commit v3 on v2

--- a/solution.py
+++ b/solution.py
@@ -264,6 +264,10 @@
         held_copy(c).wait()
 
 
+def pin(*xs):
+    return [pltpu.with_memory_space_constraint(x, pltpu.HBM) for x in xs]
+
+
 def body(acts, fresh, order, ln_gain, ln_bias, wqkv, wo):
     ticks, rows, width = fresh.shape
     n_slots = acts.shape[1]
@@ -280,11 +284,11 @@
     return pl.pallas_call(
         relay,
         out_shape=(
-            jax.ShapeDtypeStruct((ticks, 1, rows, width), bf),
-            jax.ShapeDtypeStruct((1, n_slots, rows, width), bf),
+            pltpu.VMEM((ticks, 1, rows, width), bf),
+            pltpu.VMEM((1, n_slots, rows, width), bf),
         ),
         in_specs=[anywhere, anywhere, smem, vmem, vmem, anywhere, anywhere],
-        out_specs=(anywhere, anywhere),
+        out_specs=(vmem, vmem),
         scratch_shapes=[
             pltpu.VMEM((n_slots, rows, width), bf),
             pltpu.VMEM((ticks, rows, width), bf),
@@ -312,9 +316,9 @@
             dma((ticks, n_chunks)),
         ],
         compiler_params=pltpu.CompilerParams(
-            collective_id=0, has_side_effects=True, vmem_limit_bytes=60 * 1024 * 1024
+            collective_id=0, has_side_effects=True, vmem_limit_bytes=52 * 1024 * 1024
         ),
-    )(acts, fresh, order, ln_gain, ln_bias, wqkv, wo)
+    )(*pin(acts, fresh), order, ln_gain, ln_bias, *pin(wqkv, wo))
 
 
 def solution(mesh):

time: 69.4 us -> 66.1 us (0.952)
  local copies, waits for them, and re-layouts: 4.61 us -> 1.94 us
  Pallas kernels: 64 us -> 63.3 us
    unnamed x2, local copies, waits for them, and re-layouts: 4.61 us -> 1.94 us
where the time goes in v3:
time: 66.1 us; the launch traced here: 65.9 us
  Pallas kernels  63.3 us (96%)
  local copies, waits for them, and re-layouts  1.94 us (3%)
    pallas_call x1, Pallas kernels, body(): pl.pallas_call(relay, out_shape=(pltpu.VMEM((ticks, 1, rows, width), bf),...  63.3 us
    unnamed x2, local copies, waits for them, and re-layouts  1.94 us

profile of v3, /device:TPU:1, one launch (start us, length us, event | category | flops | bytes accessed | tf_op | source)
XLA Modules:
  0.0 65.9 jit_solution(5815473592558926924)
XLA Ops:
  0.6 63.3 %shard_map.86 = (bf16[2,1,128,2048]{3,2,1,0:T(8,128)(2,1)S(1)}, bf16[1,2,128,2048]{3,2,1,0:T(8,128)(2,1)S(1)}) custom-call(bf16[1,2,128,2048]{3,2,1,0:T(8,128)(2,1)} %acts.1, bf16[2,128,2048]{2,1,0:T(8,128)(2,1)} %fresh.1, s32[1,2]{1,0:T(1,128)} %order.1, f32[1,2048]{1,0:T(1,128)} %gain.1, f32[1,2048]{1,0:T(1,128)} %bias.1, bf16[1,2048,3072]{2,1,0:T(8,128)(2,1)} %w_in.1, ...), custom_call_target="tpu_custom_call" | custom-call | tf_op jit(solution)/shard_map/pallas_call | solution.py:284
  64.0 1.0 %copy.11 = bf16[2,1,128,2048]{3,2,1,0:T(8,128)(2,1)} copy(bf16[2,1,128,2048]{3,2,1,0:T(8,128)(2,1)S(1)} %get-tuple-element.2) | data formatting | bytes 2097152
  64.9 1.0 %copy.12 = bf16[1,2,128,2048]{3,2,1,0:T(8,128)(2,1)} copy(bf16[1,2,128,2048]{3,2,1,0:T(8,128)(2,1)S(1)} %get-tuple-element.3) | data formatting | bytes 2097152

commit v4 on v3

--- a/solution.py
+++ b/solution.py
@@ -23,8 +23,8 @@
 
 def relay(
     acts, fresh, order, gain, bias, w_in, w_out, out, held,
-    slots, fresh_v, wi, wo, xs, h, qkv, mixed, part, got, res, arr,
-    acts_sem, fresh_sem, wi_sem, wo_sem, out_sem, held_sem,
+    slots, fresh_v, wi, wo, xs, h, hs, acc, qkv, mixed, part, got, arr,
+    acts_sem, fresh_sem, wi_sem, wo_sem,
     ag_send, ag_recv, rs_send, rs_recv, hop_send, hop_recv,
 ):
     ticks, rows, width = fresh.shape
@@ -77,9 +77,10 @@
         pl.semaphore_signal(barrier, inc=1, device_id={"section": sec + 1}, device_id_type=MESH)
 
     def ag_copy(t, d, c):
+        src, dst = (xs.at[t, 0], xs.at[t, d]) if t else (hs.at[0], hs.at[d])
         return pltpu.make_async_remote_copy(
-            src_ref=xs.at[t, 0, :, span(c)],
-            dst_ref=xs.at[t, d, :, span(c)],
+            src_ref=src.at[:, span(c)],
+            dst_ref=dst.at[:, span(c)],
             send_sem=ag_send.at[t, d - 1, c],
             recv_sem=ag_recv.at[t, d - 1, c],
             device_id={"tensor": lax.rem(me + d, peers)},
@@ -98,7 +99,7 @@
 
     def hop_copy(t, c):
         return pltpu.make_async_remote_copy(
-            src_ref=res.at[t, :, span(c)],
+            src_ref=out.at[t, 0, :, span(c)],
             dst_ref=arr.at[t, :, span(c)],
             send_sem=hop_send.at[t, c],
             recv_sem=hop_recv.at[t, c],
@@ -126,6 +127,7 @@
             ag_copy(t, d, c).start()
 
     def norm(t, d):
+        into = h if t else hs.at[d]
         g = gain[0:1, :]
         b = bias[0:1, :]
 
@@ -134,18 +136,32 @@
             values = xs[t, d, r, :].astype(jnp.float32)
             centred = values - jnp.mean(values, axis=-1, keepdims=True)
             spread = jnp.mean(centred * centred, axis=-1, keepdims=True)
-            h[r, :] = (centred * lax.rsqrt(spread + EPS) * g + b).astype(jnp.bfloat16)
+            into[r, :] = (centred * lax.rsqrt(spread + EPS) * g + b).astype(jnp.bfloat16)
             return carry
 
         lax.fori_loop(0, rows // NORM_ROWS, one, 0, unroll=2)
 
     def project(d, first):
+        rows_in = hs.at[0] if first else h
         for i in range(n_tiles):
             if first:
                 wi_copy(i).wait()
             cols = pl.ds(i * wi_tile, wi_tile)
-            y = jnp.dot(h[...], wi[:, cols], preferred_element_type=jnp.float32)
+            y = jnp.dot(rows_in[...], wi[:, cols], preferred_element_type=jnp.float32)
             qkv[d * rows:(d + 1) * rows, cols] = y.astype(jnp.bfloat16)
+
+    def project_chunk(d, c):
+        for i in range(n_tiles):
+            cols = pl.ds(i * wi_tile, wi_tile)
+            y = jnp.dot(
+                hs[d, :, span(c)], wi[span(c), cols], preferred_element_type=jnp.float32
+            )
+            if c:
+                y = acc[:, cols] + y
+            if c + 1 < n_chunks:
+                acc[:, cols] = y
+            else:
+                qkv[d * rows:(d + 1) * rows, cols] = y.astype(jnp.bfloat16)
 
     scale = math.log2(math.e) / math.sqrt(HD)
 
@@ -177,7 +193,7 @@
             for d in range(1, peers):
                 total = total + got[t, d - 1, r, span(c)].astype(jnp.float32)
             x = xs[t, 0, r, span(c)].astype(jnp.float32)
-            res[t, r, span(c)] = (x + total).astype(jnp.bfloat16)
+            out[t, 0, r, span(c)] = (x + total).astype(jnp.bfloat16)
 
         pieces(step)
 
@@ -187,6 +203,7 @@
 
     def take(t, c):
         chosen = order[0, t]
+        kept = slots if t + 1 < ticks else held.at[0]
 
         @pl.when(has_prev)
         def _():
@@ -196,7 +213,7 @@
             new = source[t, r, span(c)].astype(jnp.float32)
             for k in range(n_slots):
                 old = slots[k, r, span(c)].astype(jnp.float32)
-                slots[k, r, span(c)] = jnp.where(chosen == k, new, old).astype(jnp.bfloat16)
+                kept[k, r, span(c)] = jnp.where(chosen == k, new, old).astype(jnp.bfloat16)
 
         @pl.when(has_prev)
         def _():
@@ -206,15 +223,10 @@
         def _():
             pieces(functools.partial(step, source=fresh_v))
 
-    def held_copy(c):
-        return pltpu.make_async_copy(slots.at[:, :, span(c)], held.at[0, :, :, span(c)], held_sem.at[c])
-
-    def out_copy(t):
-        return pltpu.make_async_copy(res.at[t], out.at[t, 0], out_sem.at[t])
-
     for c in range(n_chunks):
         acts_copy(c).wait()
         offer(0, c)
+    norm(0, 0)
     pl.semaphore_wait(
         barrier, peers - 1 + has_prev.astype(jnp.int32) + has_next.astype(jnp.int32)
     )
@@ -222,13 +234,17 @@
         send_offer(0, c)
 
     for t in range(ticks):
-        norm(t, 0)
+        if t:
+            norm(t, 0)
         project(0, t == 0)
         for d in range(1, peers):
             for c in range(n_chunks):
                 ag_copy(t, d, c).wait_recv()
-            norm(t, d)
-            project(d, False)
+                if t == 0:
+                    project_chunk(d, c)
+            if t:
+                norm(t, d)
+                project(d, False)
         if t == 0:
             load_wo.wait()
         for d in [*range(1, peers), 0]:
@@ -239,15 +255,11 @@
         for step in range(n_chunks + lag):
             if step < n_chunks:
                 finish(t, step)
-            if step == n_chunks - 1:
-                out_copy(t).start()
             if step >= lag:
                 take(t, step - lag)
                 if t + 1 < ticks:
                     offer(t + 1, step - lag)
                     send_offer(t + 1, step - lag)
-                else:
-                    held_copy(step - lag).start()
 
     for t in range(ticks):
         for c in range(n_chunks):
@@ -258,10 +270,6 @@
             @pl.when(has_next)
             def _():
                 hop_copy(t, c).wait_send()
-
-        out_copy(t).wait()
-    for c in range(n_chunks):
-        held_copy(c).wait()
 
 
 def pin(*xs):
@@ -296,18 +304,17 @@
             pltpu.VMEM((inner, width), bf),
             pltpu.VMEM((ticks, peers, rows, width), bf),
             pltpu.VMEM((rows, width), bf),
+            pltpu.VMEM((peers, rows, width), bf),
+            pltpu.VMEM((rows, wide), jnp.float32),
             pltpu.VMEM((seq, wide), bf),
             pltpu.VMEM((rows, inner), bf),
             pltpu.VMEM((ticks, peers, rows, width), bf),
             pltpu.VMEM((ticks, peers - 1, rows, width), bf),
             pltpu.VMEM((ticks, rows, width), bf),
-            pltpu.VMEM((ticks, rows, width), bf),
             dma((n_chunks,)),
             dma,
             dma((wide // fitting(TILE, wide),)),
             dma,
-            dma((ticks,)),
-            dma((n_chunks,)),
             dma((ticks, peers - 1, n_chunks)),
             dma((ticks, peers - 1, n_chunks)),
             dma((ticks, peers - 1, n_chunks)),

time: 66.1 us -> 64.9 us (0.982)
  Pallas kernels: 63.3 us -> 62 us
    pallas_call x1, Pallas kernels: 63.3 us -> 62 us  [body(): pl.pallas_call(relay, out_shape=(pltpu.VMEM((ticks, 1, rows, width), bf),...]
where the time goes in v4:
time: 64.9 us; the launch traced here: 64.6 us
  Pallas kernels  62 us (96%)
  local copies, waits for them, and re-layouts  1.94 us (3%)
    pallas_call x1, Pallas kernels, body(): pl.pallas_call(relay, out_shape=(pltpu.VMEM((ticks, 1, rows, width), bf),...  62 us
    unnamed x2, local copies, waits for them, and re-layouts  1.94 us

profile of v4, /device:TPU:1, one launch (start us, length us, event | category | flops | bytes accessed | tf_op | source)
XLA Modules:
  0.0 64.6 jit_solution(5940965348323930031)
XLA Ops:
  0.6 62.0 %shard_map.86 = (bf16[2,1,128,2048]{3,2,1,0:T(8,128)(2,1)S(1)}, bf16[1,2,128,2048]{3,2,1,0:T(8,128)(2,1)S(1)}) custom-call(bf16[1,2,128,2048]{3,2,1,0:T(8,128)(2,1)} %acts.1, bf16[2,128,2048]{2,1,0:T(8,128)(2,1)} %fresh.1, s32[1,2]{1,0:T(1,128)} %order.1, f32[1,2048]{1,0:T(1,128)} %gain.1, f32[1,2048]{1,0:T(1,128)} %bias.1, bf16[1,2048,3072]{2,1,0:T(8,128)(2,1)} %w_in.1, ...), custom_call_target="tpu_custom_call" | custom-call | tf_op jit(solution)/shard_map/pallas_call | solution.py:292
  62.7 1.0 %copy.11 = bf16[2,1,128,2048]{3,2,1,0:T(8,128)(2,1)} copy(bf16[2,1,128,2048]{3,2,1,0:T(8,128)(2,1)S(1)} %get-tuple-element.2) | data formatting | bytes 2097152
  63.6 1.0 %copy.12 = bf16[1,2,128,2048]{3,2,1,0:T(8,128)(2,1)} copy(bf16[1,2,128,2048]{3,2,1,0:T(8,128)(2,1)S(1)} %get-tuple-element.3) | data formatting | bytes 2097152
